TPU v7x, 128 devices: a whole 4x4x4 slice. The times are simulated.
128 devices in a mesh: ex: 32 (over z, x, y_lo), feat: 4 (over y_hi, core).
Axes of the slice: x: 4, y: 4 (y_hi: 2, y_lo: 2; y = y_hi * 2 + y_lo), z: 4, core: 2. Of those that a mesh axis runs over, the one named last changes fastest.
Arguments:
- train_grads: bfloat16 [12288, 16384], P('ex', 'feat'), may hold values from -6 to 6
- projection: bfloat16 [16384, 4096], P('feat', 'ex'), may hold values from -0.046875 to 0.046875
- test_features: bfloat16 [1024, 4096], P('ex', 'feat'), may hold values from -0.09375 to 0.09375
- example_weights: float32 [12288], P('ex'), may hold values from 0.05 to 1
Outputs:
- scores: float32 [1024, 12288], P('feat', 'ex')
- projected: bfloat16 [12288, 4096], P('ex', 'feat')
All inputs are finite; a program needn't handle non-finite values.
Results may differ from a plain program's by a relative error of at most 0.0031.
Values may be sent and summed in bfloat16 or wider, within the bound.
A program may use at most 192 MiB of HBM per device.

v0:
```python
import jax
import jax.numpy as jnp
from jax import lax
from jax.sharding import Mesh
from jax.sharding import PartitionSpec as P

EX = ("ex_0", "ex_1", "ex_2")


def joined_along(pieces, dim):
    pieces = jnp.moveaxis(pieces, 0, dim)
    dims = pieces.shape
    return pieces.reshape(*dims[:dim], dims[dim] * dims[dim + 1], *dims[dim + 2 :])


def stacked_from(shard, axes, turns):
    pieces = shard[None]
    for k in turns:
        pieces = lax.all_gather(pieces, axes[k], axis=0, tiled=True)
    carried = [lax.axis_size(axes[k]) for k in reversed(turns)]
    pieces = pieces.reshape(*carried, *shard.shape)
    turned = sorted(range(len(turns)), key=lambda place: turns[len(turns) - 1 - place])
    return pieces.transpose(*turned, *range(len(turns), pieces.ndim)).reshape(-1, *shard.shape)


def gather_axes(shard, axes, turns, dim):
    return joined_along(stacked_from(shard, axes, turns), dim)


def in_blocks(shard, dim, length):
    before, after = (shard.shape[:dim], shard.shape[dim + 1 :])
    return jnp.moveaxis(shard.reshape(*before, length, -1, *after), dim, 0)


def summed_on_arrival(shard, axis, dim):
    length = lax.axis_size(axis)
    pieces = lax.all_to_all(in_blocks(shard, dim, length), axis, 0, 0, tiled=True)
    return jnp.sum(pieces, axis=0)


def local(train_grads, projection, test_features, example_weights):
    partial_value = jnp.dot(
        train_grads, gather_axes(projection, EX, (2, 0, 1), 1), preferred_element_type=jnp.float32
    )
    projected = lax.psum_scatter(partial_value, "feat", scatter_dimension=1, tiled=True).astype(
        jnp.bfloat16
    )
    partial_scores = lax.dot_general(
        lax.all_gather(test_features, EX, axis=0, tiled=True),
        projected,
        (((1,), (1,)), ((), ())),
        preferred_element_type=jnp.float32,
    )
    inner = summed_on_arrival(partial_scores, "feat", 0)
    return (inner * example_weights[None, :], projected)


def solution(mesh):
    finer = Mesh(
        mesh.devices.reshape(4, 4, 2, mesh.shape["feat"]), ("ex_0", "ex_1", "ex_2", "feat")
    )
    placed = (P(EX, "feat"), P("feat", EX), P(EX, "feat"), P(EX))
    return jax.shard_map(
        local,
        mesh=finer,
        in_specs=placed,
        out_specs=(P("feat", EX), P(EX, "feat")),
        check_vma=False,
    )
```

profile of v0, /device:TPU:1, one launch (start us, length us, event | category | flops | bytes accessed | tf_op | source)
XLA Modules:
  0.0 740.3 jit_solution(1886742789507018610)
XLA Ops:
  8.0 0.0 all-gather.12.cloned.1.call-start
  8.1 0.7 all-gather.12.cloned.1.call-update
  8.7 0.0 all-gather.6.cloned.1.call-start
  8.8 40.4 %all-gather.12.cloned.1.call-done = bf16[8192,128]{1,0:T(8,128)(2,1)} async-done(((bf16[4096,128]{1,0:T(8,128)(2,1)}), bf16[8192,128]{1,0:T(8,128)(2,1)}) %all-gather.12.cloned.1.call-update) | async-done | bytes 2097168 | tf_op jit(solution)/shard_map/all_gather | solution.py:19
  49.2 0.0 all-gather.6.cloned.1.call-update
  49.2 0.0 all-gather.8.cloned.1.call-start
  49.2 85.9 %all-gather.6.cloned.1.call-done = bf16[8,4096,128]{2,1,0:T(8,128)(2,1)} async-done(((bf16[2,4096,128]{2,1,0:T(8,128)(2,1)}), bf16[8,4096,128]{2,1,0:T(8,128)(2,1)}) %all-gather.6.cloned.1.call-update) | async-done | bytes 8388624 | tf_op jit(solution)/shard_map/all_gather | solution.py:19
  135.1 0.0 all-gather.8.cloned.1.call-update
  135.1 0.0 reduce-scatter.2.cloned.1.call-start
  135.2 296.2 %all-gather.8.cloned.1.call-done = bf16[32,4096,128]{2,1,0:T(8,128)(2,1)} async-done(((bf16[8,4096,128]{2,1,0:T(8,128)(2,1)}), bf16[32,4096,128]{2,1,0:T(8,128)(2,1)}) %all-gather.8.cloned.1.call-update) | async-done | bytes 33554448 | tf_op jit(solution)/shard_map/all_gather | solution.py:19
  431.4 22.9 %copy.9 = bf16[4,4,2,4096,128]{4,3,2,1,0:T(8,128)(2,1)} copy(bf16[4,4,2,4096,128]{4,3,2,0,1:T(8,128)(2,1)} %bitcast.18) | data formatting | bytes 67108864 | tf_op jit(solution)/shard_map/transpose | solution.py:23
  454.3 41.1 %copy.10 = bf16[4096,32,128]{0,2,1:T(8,128)(2,1)} copy(bf16[4096,32,128]{2,0,1:T(8,128)(2,1)} %bitcast.17) | data formatting | bytes 67108864 | tf_op jit(solution)/shard_map/transpose | solution.py:11
  495.4 19.8 %fusion = f32[384,4096]{1,0:T(8,128)} fusion(bf16[384,4096]{1,0:T(8,128)(2,1)S(1)} %copy-done, bf16[4096,4096]{0,1:T(8,128)(2,1)} %bitcast.19), kind=kOutput, calls=%fused_computation.2 | convolution fusion | flops 12884901888 | bytes 42991616 | tf_op jit(solution)/shard_map/dot_general | solution.py:42
  515.3 0.0 all-gather.10.cloned.1.call-start
  515.3 0.5 all-gather.10.cloned.1.call-update
  515.8 66.9 %reduce-scatter.2.cloned.1.call-done = f32[384,1024]{1,0:T(8,128)} async-done(((f32[384,4096]{1,0:T(8,128)}), f32[384,1024]{1,0:T(8,128)}) %reduce-scatter.2.cloned.1.call-update) | async-done | bytes 1572880 | tf_op jit(solution)/shard_map/reduce_scatter | solution.py:45
  582.7 1.5 convert_element_type.3
  584.3 94.7 %all-gather.10.cloned.1.call-done = bf16[1024,1024]{1,0:T(8,128)(2,1)} async-done(((bf16[32,1024]{1,0:T(8,128)(2,1)}), bf16[1024,1024]{1,0:T(8,128)(2,1)}) %all-gather.10.cloned.1.call-update) | async-done | bytes 2097168 | tf_op jit(solution)/shard_map/all_gather | solution.py:49
  679.0 2.6 fusion.1
  681.7 0.1 copy.17
  681.8 47.0 %all_to_all.5 = f32[4,256,384]{1,2,0:T(8,128)} all-to-all(f32[4,256,384]{1,2,0:T(8,128)S(1)} %bitcast.20), channel_id=1, replica_groups=mesh['ex_0'=4,'ex_1'=4,'ex_2'=2,'feat'=4] {'feat'}, dimensions={0} | all-to-all | bytes 3145728 | tf_op jit(solution)/shard_map/all_to_all | solution.py:37
  728.8 2.3 reduce_sum.9
  731.1 1.1 broadcast_multiply_fusion
  732.2 0.9 copy.13
  (9 shorter events, 0.0 us)
Async XLA Ops:
  8.0 487.4 %copy-start = (bf16[384,4096]{1,0:T(8,128)(2,1)S(1)}, bf16[384,4096]{1,0:T(8,128)(2,1)}, u32[]{:S(2)}) copy-start(bf16[384,4096]{1,0:T(8,128)(2,1)} %param.4) | copy-start | bytes 9437188
  8.0 41.1 %all-gather.12.cloned.1.call-start = ((), (), s32[]{:S(2)}) async-start(), calls=%async_computation.6 | async-start | bytes 3145728 | tf_op jit(solution)/shard_map/all_gather | solution.py:19
  8.7 126.4 %all-gather.6.cloned.1.call-start = ((), (), s32[]{:S(2)}) async-start(), calls=%async_computation.2 | async-start | bytes 10485760 | tf_op jit(solution)/shard_map/all_gather | solution.py:19
  49.2 382.2 %all-gather.8.cloned.1.call-start = ((), (), s32[]{:S(2)}) async-start(), calls=%async_computation.3 | async-start | bytes 41943040 | tf_op jit(solution)/shard_map/all_gather | solution.py:19
  135.1 447.6 %reduce-scatter.2.cloned.1.call-start = ((), (), s32[]{:S(2)}) async-start(), calls=%async_computation.4 | async-start | bytes 7864320 | tf_op jit(solution)/shard_map/reduce_scatter | solution.py:45
  515.3 163.8 %all-gather.10.cloned.1.call-start = ((), (), s32[]{:S(2)}) async-start(), calls=%async_computation.5 | async-start | bytes 2162688 | tf_op jit(solution)/shard_map/all_gather | solution.py:49
  584.3 97.4 %copy-start.2 = (bf16[384,1024]{1,0:T(8,128)(2,1)}, bf16[384,1024]{1,0:T(8,128)(2,1)S(1)}, u32[]{:S(2)}) copy-start(bf16[384,1024]{1,0:T(8,128)(2,1)S(1)} %convert_element_type.3) | copy-start | bytes 2359300
  681.8 49.3 %copy-start.3 = (f32[384]{0:T(512)S(1)}, f32[384]{0:T(512)}, u32[]{:S(2)}) copy-start(f32[384]{0:T(512)} %param.7) | copy-start | bytes 4612
  681.8 51.3 %copy-start.1 = (bf16[384,4096]{1,0:T(8,128)(2,1)S(1)}, bf16[384,4096]{1,0:T(8,128)(2,1)}, u32[]{:S(2)}) copy-start(bf16[384,4096]{1,0:T(8,128)(2,1)} %param.4) | copy-start | bytes 9437188
Sparse Core Ops, SparseCore 0:
  10.5 38.6 all-gather.11
  50.8 84.2 all-gather.5
  136.8 294.5 all-gather.7
  515.4 67.3 reduce-scatter.1
Sparse Core Ops, SparseCore 1:
  517.4 161.6 all-gather.9
where the time goes:
time: 742 us; the launch traced here: 740 us
  waiting for transfers between devices  585 us (79%)
  local copies, waits for them, and re-layouts  65.1 us (9%)
  blocking collectives  47 us (6%)
  matrix products  22.4 us (3%)
  between operations  15.3 us (2%)
    all_gather x3, waiting for transfers between devices, stacked_from(): pieces = lax.all_gather(pieces, axes[k], axis=0, tiled=True)  422 us
    all_gather x1, waiting for transfers between devices, local(): lax.all_gather(test_features, EX, axis=0, tiled=True)  94.7 us
    reduce_scatter x1, waiting for transfers between devices, local(): lax.psum_scatter(partial_value, 'feat', scatter_dimension=1, tiled=True)  66.9 us
    all_to_all x1, blocking collectives, summed_on_arrival(): lax.all_to_all(in_blocks(shard, dim, length), axis, 0, 0, tiled=True)  47 us
    transpose x1, local copies, waits for them, and re-layouts, joined_along(): pieces = jnp.moveaxis(pieces, 0, dim)  41.1 us
    transpose x1, local copies, waits for them, and re-layouts, stacked_from(): pieces.transpose(*turned, *range(len(turns), pieces.ndim))  22.9 us
    dot_general x1, matrix products, local(): jnp.dot(train_grads, gather_axes(projection, EX, (2, 0, 1), 1), preferred...  19.8 us
  transfers between devices with their start and end apart: 5, of which 5 were waited for; matrix products, arithmetic and copies ran while one was open for 0% of the time, Pallas kernels for 0%

commit v1 on v0

v1 whole, which is shorter than its diff:
```python
import functools

import jax
import jax.numpy as jnp
from jax import lax
from jax.experimental import pallas as pl
from jax.experimental.pallas import tpu as pltpu
from jax.sharding import PartitionSpec as P

MESH = pl.DeviceIdType.MESH
ROWS = 384
DEPTH = 4096
HALF = DEPTH // 2
QUARTER = HALF // 2
LANES = 128
STEP = 512


def project_kernel(
    g_hbm, r_hbm, out_ref, buf, gbuf, cst, xrecv, pst, rcv,
    local_sem, send_sem, piece_sem, g_sem, x_sem, rcv_sem,
):
    ex = lax.axis_index("ex")
    ft = lax.axis_index("feat")
    z, x, yl = ex // 8, (ex // 2) % 4, ex % 2
    yh, c = ft // 2, ft % 2

    def at(dx=0, dz=0, flip_lo=0, flip_hi=0, flip_core=0):
        lo = 1 - yl if flip_lo else yl
        hi = 1 - yh if flip_hi else yh
        core = 1 - c if flip_core else c
        return (((z + dz) % 4) * 8 + ((x + dx) % 4) * 2 + lo, hi * 2 + core)

    first = ("x", "z")
    second = ("z", "x")

    def neighbour(axis, way):
        return at(dx=way) if axis == "x" else at(dz=way)

    pair, twin, opposite, diagonal = (
        at(flip_lo=1), at(flip_core=1), at(flip_hi=1), at(flip_lo=1, flip_hi=1)
    )
    sent = []

    def send(src, dst, sem, device):
        copy = pltpu.make_async_remote_copy(
            src, dst, send_sem.at[len(sent)], sem, device_id=device, device_id_type=MESH
        )
        copy.start()
        sent.append(copy)

    own_r = []
    for h in range(2):
        copy = pltpu.make_async_copy(
            r_hbm.at[pl.ds(h * HALF, HALF)], buf.at[h, 0, 0], local_sem.at[h]
        )
        copy.start()
        own_r.append(copy)
    own_g = pltpu.make_async_copy(g_hbm, gbuf.at[0], local_sem.at[2])
    own_g.start()

    barrier = pltpu.get_barrier_semaphore()
    friends = [at(dx=1), at(dx=-1), at(dz=1), at(dz=-1), pair, twin, opposite, diagonal]
    for device in friends:
        pl.semaphore_signal(barrier, inc=1, device_id=device, device_id_type=MESH)
    pl.semaphore_wait(barrier, len(friends))

    def sem_of(h, a, b):
        return piece_sem.at[h * 16 + a * 4 + b]

    def hop(h, axis, a, b, way, part=None):
        if axis == 0:
            a2, b2 = (a + way) % 4, b
        else:
            a2, b2 = a, (b + way) % 4
        src, dst = buf.at[h, a, b], buf.at[h, a2, b2]
        if part is not None:
            rows = pl.ds(part * QUARTER, QUARTER)
            src, dst = src.at[rows], dst.at[rows]
        send(src, dst, sem_of(h, a2, b2), neighbour((first, second)[axis][h], way))

    def arrived(h, a, b):
        ref = buf.at[h, a, b]
        pltpu.make_async_remote_copy(
            ref, ref, send_sem.at[0], sem_of(h, a, b), device_id=twin, device_id_type=MESH
        ).wait_recv()

    def each(a, b):
        for h in range(2):
            arrived(h, a, b)

    for h in range(2):
        own_r[h].wait()
        for way in (1, -1):
            hop(h, 0, 0, 0, way)
    for h in range(2):
        for way in (1, -1):
            hop(h, 1, 0, 0, way)
    own_g.wait()
    send(gbuf.at[0], gbuf.at[1], g_sem.at[0], pair)

    mine = (c + z) % 2
    keeps_first = ((z - mine + 4) % 4) // 2 == yh
    kept = jnp.where(keeps_first, 0, 1)

    def multiply(s, dx, p):
        item = dx * 2 + p

        def rows_at(i, carry):
            rows = pl.ds(pl.multiple_of(i * LANES, LANES), LANES)
            acc = jnp.zeros((LANES, 2 * LANES), jnp.float32)
            for h in range(2):
                for k in range(0, HALF, STEP):
                    ks = pl.ds(k, STEP)
                    pieces = [
                        buf[0, dx, 2 * p + i, ks, :] if h == 0 else buf[1, 2 * p + i, dx, ks, :]
                        for i in range(2)
                    ]
                    acc += jnp.dot(
                        gbuf[s, rows, pl.ds(h * HALF + k, STEP)],
                        jnp.concatenate(pieces, axis=1),
                        preferred_element_type=jnp.float32,
                    )
            cst[s, item, 0, rows, :] = acc[:, :LANES]
            cst[s, item, 1, rows, :] = acc[:, LANES:]
            return carry

        lax.fori_loop(0, ROWS // LANES, rows_at, 0)
        send(cst.at[s, item, 1 - mine], xrecv.at[s, item], x_sem.at[s * 8 + item], twin)

    given = []

    def add_twin(s, dx, p):
        item = dx * 2 + p
        ref = xrecv.at[s, item]
        pltpu.make_async_remote_copy(
            ref, ref, send_sem.at[0], x_sem.at[s * 8 + item], device_id=twin, device_id_type=MESH
        ).wait_recv()
        total = cst[s, item, mine] + xrecv[s, item]
        pst[s, item] = total.astype(jnp.bfloat16)
        keep = kept == p
        if s == 0:
            cst[s, item, mine] = total
            copy = pltpu.make_async_remote_copy(
                pst.at[s, item], rcv.at[0, dx], send_sem.at[len(sent)], rcv_sem.at[dx],
                device_id=opposite, device_id_type=MESH,
            )
            sent.append(None)

            @pl.when(jnp.logical_not(keep))
            def _():
                copy.start()

            given.append((copy, keep))
        else:
            slot = jnp.where(keep, 1, 2)
            hi = jnp.where(keep, yh, 1 - yh)
            send(
                pst.at[s, item], rcv.at[slot, dx], rcv_sem.at[slot * 4 + dx],
                (pair[0], hi * 2 + c),
            )

    def finish(dx):
        for k in range(3):
            ref = rcv.at[k, dx]
            pltpu.make_async_remote_copy(
                ref, ref, send_sem.at[0], rcv_sem.at[k * 4 + dx], device_id=twin, device_id_type=MESH
            ).wait_recv()
        chunk = ((x - dx + 4) % 4) * 2
        own = cst[0, dx * 2 + kept, mine] + rcv[0, dx].astype(jnp.float32)
        other = rcv[1, dx].astype(jnp.float32) + rcv[2, dx].astype(jnp.float32)
        lanes = pl.ds(pl.multiple_of((chunk + yl) * LANES, LANES), LANES)
        out_ref[:, lanes] = own.astype(jnp.bfloat16)
        lanes = pl.ds(pl.multiple_of((chunk + 1 - yl) * LANES, LANES), LANES)
        out_ref[:, lanes] = other.astype(jnp.bfloat16)

    each(1, 0)
    each(3, 0)
    for h in range(2):
        hop(h, 0, 1, 0, 1, part=0)
        hop(h, 0, 3, 0, -1, part=1)
    for a in (1, 3):
        for h in range(2):
            for way in (1, -1):
                hop(h, 1, a, 0, way)
    each(0, 1)
    each(0, 3)
    for h in range(2):
        hop(h, 1, 0, 1, 1, part=0)
        hop(h, 1, 0, 3, -1, part=1)
    multiply(0, 0, 0)
    each(2, 0)
    for h in range(2):
        for way in (1, -1):
            hop(h, 1, 2, 0, way)
    add_twin(0, 0, 0)
    for a in (1, 3):
        each(a, 1)
        each(a, 3)
        for h in range(2):
            hop(h, 1, a, 1, 1, part=0)
            hop(h, 1, a, 3, -1, part=1)
        if a == 1:
            multiply(0, 1, 0)
    add_twin(0, 1, 0)
    multiply(0, 3, 0)
    each(0, 2)
    multiply(0, 0, 1)
    add_twin(0, 3, 0)
    each(2, 1)
    each(2, 3)
    for h in range(2):
        hop(h, 1, 2, 1, 1, part=0)
        hop(h, 1, 2, 3, -1, part=1)
    add_twin(0, 0, 1)
    each(1, 2)
    multiply(0, 2, 0)
    multiply(0, 1, 1)
    add_twin(0, 2, 0)
    add_twin(0, 1, 1)
    ref = gbuf.at[1]
    pltpu.make_async_remote_copy(
        ref, ref, send_sem.at[0], g_sem.at[0], device_id=twin, device_id_type=MESH
    ).wait_recv()
    before = None
    for now in ((0, 0), (0, 1), (1, 0), (1, 1), (3, 0), (2, 0)):
        multiply(1, *now)
        if before is not None:
            add_twin(1, *before)
        before = now
    each(3, 2)
    multiply(0, 3, 1)
    add_twin(1, *before)
    multiply(1, 3, 1)
    add_twin(0, 3, 1)
    finish(0)
    add_twin(1, 3, 1)
    finish(1)
    each(2, 2)
    multiply(0, 2, 1)
    multiply(1, 2, 1)
    add_twin(0, 2, 1)
    add_twin(1, 2, 1)
    finish(3)
    finish(2)
    for copy in sent:
        if copy is not None:
            copy.wait_send()
    for copy, keep in given:
        @pl.when(jnp.logical_not(keep))
        def _():
            copy.wait_send()


def project(train_grads, projection):
    flops = 2 * 2 * ROWS * DEPTH * 2048
    return pl.pallas_call(
        project_kernel,
        out_shape=jax.ShapeDtypeStruct((ROWS, 1024), jnp.bfloat16),
        in_specs=[pl.BlockSpec(memory_space=pl.ANY)] * 2,
        out_specs=pl.BlockSpec(memory_space=pltpu.VMEM),
        scratch_shapes=[
            pltpu.VMEM((2, 4, 4, HALF, LANES), jnp.bfloat16),
            pltpu.VMEM((2, ROWS, DEPTH), jnp.bfloat16),
            pltpu.VMEM((2, 8, 2, ROWS, LANES), jnp.float32),
            pltpu.VMEM((2, 8, ROWS, LANES), jnp.float32),
            pltpu.VMEM((2, 8, ROWS, LANES), jnp.bfloat16),
            pltpu.VMEM((3, 4, ROWS, LANES), jnp.bfloat16),
            pltpu.SemaphoreType.DMA((3,)),
            pltpu.SemaphoreType.DMA((96,)),
            pltpu.SemaphoreType.DMA((32,)),
            pltpu.SemaphoreType.DMA((1,)),
            pltpu.SemaphoreType.DMA((16,)),
            pltpu.SemaphoreType.DMA((12,)),
        ],
        compiler_params=pltpu.CompilerParams(
            collective_id=0, has_side_effects=True, vmem_limit_bytes=60 * 1024 * 1024
        ),
        cost_estimate=pl.CostEstimate(
            flops=flops * 8, bytes_accessed=8 * 2**20, transcendentals=0
        ),
    )(train_grads, projection)


def local(train_grads, projection, test_features, example_weights):
    projected = project(train_grads, projection)
    tests = lax.all_gather(test_features, "ex", axis=0, tiled=True)
    partial_scores = lax.dot_general(
        tests, projected, (((1,), (1,)), ((), ())), preferred_element_type=jnp.float32
    )
    pieces = lax.all_to_all(partial_scores.reshape(4, 256, ROWS), "feat", 0, 0, tiled=True)
    return jnp.sum(pieces, axis=0) * example_weights[None, :], projected


def solution(mesh):
    return jax.shard_map(
        local,
        mesh=mesh,
        in_specs=(P("ex", "feat"), P("feat", "ex"), P("ex", "feat"), P("ex")),
        out_specs=(P("feat", "ex"), P("ex", "feat")),
        check_vma=False,
    )
```

time: 742 us -> 206 us (0.28)
  waiting for transfers between devices: 585 us -> 5.48 us
  Pallas kernels: 0 us -> 138 us
  local copies, waits for them, and re-layouts: 65.1 us -> 1.92 us
  matrix products: 22.4 us -> 2.85 us
    all_gather x4 -> x1, waiting for transfers between devices: 517 us -> 4.8 us  [local(): tests = lax.all_gather(test_features, 'ex', axis=0, tiled=True)]
    pallas_call x0 -> x1, Pallas kernels: none -> 138 us  [project(): pl.pallas_call(project_kernel, out_shape=jax.ShapeDtypeStruct((ROWS, 1024...]
    reduce_scatter x1 -> x0, waiting for transfers between devices: 66.9 us -> none  [local(): lax.psum_scatter(partial_value, 'feat', scatter_dimension=1, tiled=True)]
    transpose x2 -> x0, local copies, waits for them, and re-layouts: 64 us -> none  [the longest x1 41.1 us: joined_along(): pieces = jnp.moveaxis(pieces, 0, dim)]
    dot_general x2 -> x1, matrix products: 22.4 us -> 2.85 us  [local(): lax.dot_general(tests, projected, (((1,), (1,)), ((), ())), preferred_ele...]
  transfers between devices with their start and end apart: 5 -> 1, of which waited for: 5 -> 1; matrix products, arithmetic and copies ran while one was open for 0% -> 0% of each run, Pallas kernels for 0% -> 67%
where the time goes in v1:
time: 206 us
  Pallas kernels  138 us (67%)
  blocking collectives  44.1 us (21%)
  between operations  14.1 us (7%)
  waiting for transfers between devices  5.48 us (3%)
  matrix products  2.85 us (1%)
    pallas_call x1, Pallas kernels, project(): pl.pallas_call(project_kernel, out_shape=jax.ShapeDtypeStruct((ROWS, 1024...  138 us
    all_to_all x1, blocking collectives, local(): lax.all_to_all(partial_scores.reshape(4, 256, ROWS), 'feat', 0, 0, tiled=...  44.1 us
    all_gather x1, waiting for transfers between devices, local(): tests = lax.all_gather(test_features, 'ex', axis=0, tiled=True)  4.8 us
  transfers between devices with their start and end apart: 1, of which 1 were waited for; matrix products, arithmetic and copies ran while one was open for 0% of the time, Pallas kernels for 67%

profile of v1, /device:TPU:1, one launch (start us, length us, event | category | flops | bytes accessed | tf_op | source)
XLA Modules:
  0.0 206.3 jit_solution(12959992382536627822)
XLA Ops:
  7.2 0.0 all-gather.2.cloned.1.call-start
  7.2 0.7 all-gather.2.cloned.1.call-update
  7.9 137.6 %shard_map.59 = bf16[384,1024]{1,0:T(8,128)(2,1)} custom-call(bf16[384,4096]{1,0:T(8,128)(2,1)} %g_hbm.1, bf16[4096,128]{1,0:T(8,128)(2,1)} %r_hbm.1), custom_call_target="tpu_custom_call" | custom-call | flops 103079215104 | bytes 8388608 | tf_op jit(solution)/shard_map/pallas_call | solution.py:257
  145.5 4.8 %all-gather.2.cloned.1.call-done = bf16[1024,1024]{1,0:T(8,128)(2,1)} async-done(((bf16[32,1024]{1,0:T(8,128)(2,1)}), bf16[1024,1024]{1,0:T(8,128)(2,1)}) %all-gather.2.cloned.1.call-update) | async-done | bytes 2097168 | tf_op jit(solution)/shard_map/all_gather | solution.py:287
  150.3 2.9 %fusion = f32[384,1024]{1,0:T(8,128)S(1)} fusion(bf16[384,1024]{1,0:T(8,128)(2,1)} %shard_map.59, bf16[1024,1024]{1,0:T(8,128)(2,1)} %all-gather.2.cloned.1.call-done), kind=kOutput, calls=%fused_computation.2 | convolution fusion | flops 805306368 | bytes 4456448 | tf_op jit(solution)/shard_map/dot_general | solution.py:288
  153.1 0.1 copy.12
  153.3 0.0 copy-start.1
  153.3 44.1 %all_to_all.5 = f32[4,256,384]{1,2,0:T(8,128)S(1)} all-to-all(f32[4,256,384]{1,2,0:T(8,128)S(1)} %bitcast.7), channel_id=1, replica_groups=mesh['ex'=32,'feat'=4] {'feat'}, dimensions={0} | all-to-all | bytes 3145728 | tf_op jit(solution)/shard_map/all_to_all | solution.py:291
  197.4 0.0 copy-start
  197.4 0.1 reduce_sum.9
  197.5 0.0 copy-done.1
  197.5 0.1 broadcast_multiply_fusion
  197.6 0.9 copy.8
  198.5 0.0 copy-done
  198.5 0.9 copy.14
Async XLA Ops:
  7.2 143.1 %all-gather.2.cloned.1.call-start = ((), (), s32[]{:S(2)}) async-start(), calls=%async_computation.1 | async-start | bytes 2162688 | tf_op jit(solution)/shard_map/all_gather | solution.py:287
  153.3 44.2 %copy-start.1 = (f32[384]{0:T(512)S(1)}, f32[384]{0:T(512)}, u32[]{:S(2)}) copy-start(f32[384]{0:T(512)} %param.7) | copy-start | bytes 4612
  197.4 1.2 copy-start
Sparse Core Ops, SparseCore 0:
  9.6 140.6 all-gather.1

commit v2 on v1

--- a/solution.py
+++ b/solution.py
@@ -1,5 +1,3 @@
-import functools
-
 import jax
 import jax.numpy as jnp
 from jax import lax
@@ -9,6 +7,7 @@
 
 MESH = pl.DeviceIdType.MESH
 ROWS = 384
+TESTS = 32
 DEPTH = 4096
 HALF = DEPTH // 2
 QUARTER = HALF // 2
@@ -17,8 +16,9 @@
 
 
 def project_kernel(
-    g_hbm, r_hbm, out_ref, buf, gbuf, cst, xrecv, pst, rcv,
-    local_sem, send_sem, piece_sem, g_sem, x_sem, rcv_sem,
+    g_hbm, r_hbm, t_hbm, w_ref, score_ref, out_ref, buf, gbuf, cst, xrecv, pst, rcv,
+    tall, part_scores, twin_scores, far_scores,
+    local_sem, send_sem, piece_sem, g_sem, x_sem, rcv_sem, t_sem, score_sem,
 ):
     ex = lax.axis_index("ex")
     ft = lax.axis_index("feat")
@@ -58,6 +58,17 @@
         own_r.append(copy)
     own_g = pltpu.make_async_copy(g_hbm, gbuf.at[0], local_sem.at[2])
     own_g.start()
+
+    def test_rows(h, a, b):
+        dx, dz = (a, b) if h == 0 else (b, a)
+        lo = yl if h == 0 else 1 - yl
+        source = ((z - dz + 4) % 4) * 8 + ((x - dx + 4) % 4) * 2 + lo
+        return pl.multiple_of(source * TESTS, TESTS)
+
+    own_t = pltpu.make_async_copy(
+        t_hbm, tall.at[pl.ds(test_rows(0, 0, 0), TESTS)], local_sem.at[3]
+    )
+    own_t.start()
 
     barrier = pltpu.get_barrier_semaphore()
     friends = [at(dx=1), at(dx=-1), at(dz=1), at(dz=-1), pair, twin, opposite, diagonal]
@@ -85,6 +96,24 @@
             ref, ref, send_sem.at[0], sem_of(h, a, b), device_id=twin, device_id_type=MESH
         ).wait_recv()
 
+    def test_hop(h, axis, a, b, way, part=None):
+        a2, b2 = ((a + way) % 4, b) if axis == 0 else (a, (b + way) % 4)
+        start, count = test_rows(h, a, b), TESTS
+        if part is not None:
+            start, count = pl.multiple_of(start + part * (TESTS // 2), TESTS // 2), TESTS // 2
+        rows = pl.ds(start, count)
+        send(
+            tall.at[rows], tall.at[rows], t_sem.at[h * 16 + a2 * 4 + b2],
+            neighbour((first, second)[axis][h], way),
+        )
+
+    def tests_arrived(h, a, b):
+        ref = tall.at[pl.ds(test_rows(h, a, b), TESTS)]
+        pltpu.make_async_remote_copy(
+            ref, ref, send_sem.at[0], t_sem.at[h * 16 + a * 4 + b], device_id=twin,
+            device_id_type=MESH,
+        ).wait_recv()
+
     def each(a, b):
         for h in range(2):
             arrived(h, a, b)
@@ -96,6 +125,9 @@
     for h in range(2):
         for way in (1, -1):
             hop(h, 1, 0, 0, way)
+    own_t.wait()
+    rows = pl.ds(test_rows(0, 0, 0), TESTS)
+    send(tall.at[rows], tall.at[rows], t_sem.at[16], pair)
     own_g.wait()
     send(gbuf.at[0], gbuf.at[1], g_sem.at[0], pair)
 
@@ -188,6 +220,11 @@
     for h in range(2):
         hop(h, 1, 0, 1, 1, part=0)
         hop(h, 1, 0, 3, -1, part=1)
+    tests_arrived(1, 0, 0)
+    for axis in range(2):
+        for h in range(2):
+            for way in (1, -1):
+                test_hop(h, axis, 0, 0, way)
     multiply(0, 0, 0)
     each(2, 0)
     for h in range(2):
@@ -202,6 +239,13 @@
             hop(h, 1, a, 3, -1, part=1)
         if a == 1:
             multiply(0, 1, 0)
+    for a in (1, 3):
+        for h in range(2):
+            tests_arrived(h, a, 0)
+            tests_arrived(h, 0, a)
+            way = 1 if a == 1 else -1
+            test_hop(h, 0, a, 0, way, part=a // 2)
+            test_hop(h, 1, 0, a, way, part=a // 2)
     add_twin(0, 1, 0)
     multiply(0, 3, 0)
     each(0, 2)
@@ -212,6 +256,12 @@
     for h in range(2):
         hop(h, 1, 2, 1, 1, part=0)
         hop(h, 1, 2, 3, -1, part=1)
+    for h in range(2):
+        tests_arrived(h, 2, 0)
+    for a in (1, 3, 2):
+        for h in range(2):
+            for way in (1, -1):
+                test_hop(h, 1, a, 0, way)
     add_twin(0, 0, 1)
     each(1, 2)
     multiply(0, 2, 0)
@@ -237,12 +287,57 @@
     add_twin(1, 3, 1)
     finish(1)
     each(2, 2)
+    for a in (1, 3, 2):
+        for h in range(2):
+            tests_arrived(h, a, 1)
+            tests_arrived(h, a, 3)
+            test_hop(h, 1, a, 1, 1, part=0)
+            test_hop(h, 1, a, 3, -1, part=1)
     multiply(0, 2, 1)
     multiply(1, 2, 1)
     add_twin(0, 2, 1)
     add_twin(1, 2, 1)
     finish(3)
+    for h in range(2):
+        for a in range(4):
+            tests_arrived(h, a, 2)
     finish(2)
+
+    def score(quarter):
+        def tile(i, carry):
+            rows = pl.ds(pl.multiple_of(quarter * 256 + i * LANES, LANES), LANES)
+            part_scores[quarter, pl.ds(pl.multiple_of(i * LANES, LANES), LANES), :] = (
+                lax.dot_general(
+                    tall[rows, :], out_ref[...], (((1,), (1,)), ((), ())),
+                    preferred_element_type=jnp.float32,
+                )
+            )
+            return carry
+
+        lax.fori_loop(0, 2, tile, 0)
+
+    def twin_sum(quarter, k):
+        ref = twin_scores.at[k]
+        pltpu.make_async_remote_copy(
+            ref, ref, send_sem.at[0], score_sem.at[k], device_id=twin, device_id_type=MESH
+        ).wait_recv()
+        return part_scores[quarter] + twin_scores[k]
+
+    far, near = (1 - yh) * 2, yh * 2
+    score(far + 1 - c)
+    send(part_scores.at[far + 1 - c], twin_scores.at[0], score_sem.at[0], twin)
+    score(far + c)
+    part_scores[far + c] = twin_sum(far + c, 0)
+    send(part_scores.at[far + c], far_scores, score_sem.at[2], opposite)
+    score(near + 1 - c)
+    send(part_scores.at[near + 1 - c], twin_scores.at[1], score_sem.at[1], twin)
+    score(near + c)
+    total = twin_sum(near + c, 1)
+    pltpu.make_async_remote_copy(
+        far_scores, far_scores, send_sem.at[0], score_sem.at[2], device_id=twin,
+        device_id_type=MESH,
+    ).wait_recv()
+    score_ref[...] = (total + far_scores[...]) * w_ref[...]
     for copy in sent:
         if copy is not None:
             copy.wait_send()
@@ -252,13 +347,17 @@
             copy.wait_send()
 
 
-def project(train_grads, projection):
+def local(train_grads, projection, test_features, example_weights):
     flops = 2 * 2 * ROWS * DEPTH * 2048
     return pl.pallas_call(
         project_kernel,
-        out_shape=jax.ShapeDtypeStruct((ROWS, 1024), jnp.bfloat16),
-        in_specs=[pl.BlockSpec(memory_space=pl.ANY)] * 2,
-        out_specs=pl.BlockSpec(memory_space=pltpu.VMEM),
+        out_shape=(
+            jax.ShapeDtypeStruct((256, ROWS), jnp.float32),
+            jax.ShapeDtypeStruct((ROWS, 1024), jnp.bfloat16),
+        ),
+        in_specs=[pl.BlockSpec(memory_space=pl.ANY)] * 3
+        + [pl.BlockSpec(memory_space=pltpu.VMEM)],
+        out_specs=(pl.BlockSpec(memory_space=pltpu.VMEM),) * 2,
         scratch_shapes=[
             pltpu.VMEM((2, 4, 4, HALF, LANES), jnp.bfloat16),
             pltpu.VMEM((2, ROWS, DEPTH), jnp.bfloat16),
@@ -266,30 +365,26 @@
             pltpu.VMEM((2, 8, ROWS, LANES), jnp.float32),
             pltpu.VMEM((2, 8, ROWS, LANES), jnp.bfloat16),
             pltpu.VMEM((3, 4, ROWS, LANES), jnp.bfloat16),
-            pltpu.SemaphoreType.DMA((3,)),
-            pltpu.SemaphoreType.DMA((96,)),
+            pltpu.VMEM((1024, 1024), jnp.bfloat16),
+            pltpu.VMEM((4, 256, ROWS), jnp.float32),
+            pltpu.VMEM((2, 256, ROWS), jnp.float32),
+            pltpu.VMEM((256, ROWS), jnp.float32),
+            pltpu.SemaphoreType.DMA((4,)),
+            pltpu.SemaphoreType.DMA((136,)),
             pltpu.SemaphoreType.DMA((32,)),
             pltpu.SemaphoreType.DMA((1,)),
             pltpu.SemaphoreType.DMA((16,)),
             pltpu.SemaphoreType.DMA((12,)),
+            pltpu.SemaphoreType.DMA((32,)),
+            pltpu.SemaphoreType.DMA((3,)),
         ],
         compiler_params=pltpu.CompilerParams(
             collective_id=0, has_side_effects=True, vmem_limit_bytes=60 * 1024 * 1024
         ),
         cost_estimate=pl.CostEstimate(
-            flops=flops * 8, bytes_accessed=8 * 2**20, transcendentals=0
+            flops=flops, bytes_accessed=8 * 2**20, transcendentals=0
         ),
-    )(train_grads, projection)
-
-
-def local(train_grads, projection, test_features, example_weights):
-    projected = project(train_grads, projection)
-    tests = lax.all_gather(test_features, "ex", axis=0, tiled=True)
-    partial_scores = lax.dot_general(
-        tests, projected, (((1,), (1,)), ((), ())), preferred_element_type=jnp.float32
-    )
-    pieces = lax.all_to_all(partial_scores.reshape(4, 256, ROWS), "feat", 0, 0, tiled=True)
-    return jnp.sum(pieces, axis=0) * example_weights[None, :], projected
+    )(train_grads, projection, test_features, example_weights.reshape(1, ROWS))
 
 
 def solution(mesh):

time: 206 us -> 148 us (0.72)
  the two profiles are of different devices: /device:TPU:1 before, /device:TPU:45 now
where the time goes in v2:
time: 148 us; the launch traced here: 147 us
  Pallas kernels  142 us (96%)
  local copies, waits for them, and re-layouts  5.07 us (3%)
    pallas_call x1, Pallas kernels, local(): pl.pallas_call(project_kernel, out_shape=(jax.ShapeDtypeStruct((256, ROWS...  142 us
    unnamed x2, local copies, waits for them, and re-layouts  3.83 us

profile of v2, /device:TPU:45, one launch (start us, length us, event | category | flops | bytes accessed | tf_op | source)
XLA Modules:
  0.0 147.4 jit_solution(12133199359919930858)
XLA Ops:
  0.6 1.2 reshape.7.w_ref
  1.9 141.7 %shard_map.59 = (f32[256,384]{1,0:T(8,128)}, bf16[384,1024]{1,0:T(8,128)(2,1)}) custom-call(bf16[384,4096]{1,0:T(8,128)(2,1)} %g_hbm.1, bf16[4096,128]{1,0:T(8,128)(2,1)} %r_hbm.1, bf16[32,1024]{1,0:T(8,128)(2,1)} %t_hbm.1, f32[1,384]{1,0:T(1,128)} %reshape.7.w_ref), custom_call_target="tpu_custom_call" | custom-call | flops 12884901888 | bytes 8388608 | tf_op jit(solution)/shard_map/pallas_call | solution.py:352
  143.6 1.8 %copy.8 = f32[256,384]{1,0:T(8,128)} copy(f32[256,384]{1,0:T(8,128)} %get-tuple-element.4) | data formatting | bytes 786432
  145.4 2.1 %copy.9 = bf16[384,1024]{1,0:T(8,128)(2,1)} copy(bf16[384,1024]{1,0:T(8,128)(2,1)} %get-tuple-element.5) | data formatting | bytes 1572864

commit v3 on v2

--- a/solution.py
+++ b/solution.py
@@ -8,6 +8,8 @@
 MESH = pl.DeviceIdType.MESH
 ROWS = 384
 TESTS = 32
+TILE = 192
+TILES = ROWS // TILE
 DEPTH = 4096
 HALF = DEPTH // 2
 QUARTER = HALF // 2
@@ -16,8 +18,8 @@
 
 
 def project_kernel(
-    g_hbm, r_hbm, t_hbm, w_ref, score_ref, out_ref, buf, gbuf, cst, xrecv, pst, rcv,
-    tall, part_scores, twin_scores, far_scores,
+    g_hbm, r_hbm, t_hbm, score_ref, out_ref, buf, gbuf, cst, xrecv, pst, rcv,
+    tall, part_scores, twin_scores, relay_scores, far_scores,
     local_sem, send_sem, piece_sem, g_sem, x_sem, rcv_sem, t_sem, score_sem,
 ):
     ex = lax.axis_index("ex")
@@ -114,6 +116,11 @@
             device_id_type=MESH,
         ).wait_recv()
 
+    def landed(ref, sem):
+        pltpu.make_async_remote_copy(
+            ref, ref, send_sem.at[0], sem, device_id=twin, device_id_type=MESH
+        ).wait_recv()
+
     def each(a, b):
         for h in range(2):
             arrived(h, a, b)
@@ -129,38 +136,47 @@
     rows = pl.ds(test_rows(0, 0, 0), TESTS)
     send(tall.at[rows], tall.at[rows], t_sem.at[16], pair)
     own_g.wait()
-    send(gbuf.at[0], gbuf.at[1], g_sem.at[0], pair)
+    for t in range(TILES):
+        rows = pl.ds(t * TILE, TILE)
+        send(gbuf.at[0, rows], gbuf.at[1, rows], g_sem.at[t], pair)
 
     mine = (c + z) % 2
     keeps_first = ((z - mine + 4) % 4) // 2 == yh
     kept = jnp.where(keeps_first, 0, 1)
 
+    def tile(s, dx, p, t):
+        item = dx * 2 + p
+        rows = pl.ds(pl.multiple_of(t * TILE, TILE), TILE)
+        acc = jnp.zeros((TILE, 2 * LANES), jnp.float32)
+        for h in range(2):
+            for k in range(0, HALF, STEP):
+                ks = pl.ds(k, STEP)
+                pieces = [
+                    buf[0, dx, 2 * p + i, ks, :] if h == 0 else buf[1, 2 * p + i, dx, ks, :]
+                    for i in range(2)
+                ]
+                acc += jnp.dot(
+                    gbuf[s, rows, pl.ds(h * HALF + k, STEP)],
+                    jnp.concatenate(pieces, axis=1),
+                    preferred_element_type=jnp.float32,
+                )
+        cst[s, item, 0, rows, :] = acc[:, :LANES]
+        cst[s, item, 1, rows, :] = acc[:, LANES:]
+
+    def to_other_core(s, dx, p):
+        item = dx * 2 + p
+        send(cst.at[s, item, 1 - mine], xrecv.at[s, item], x_sem.at[s * 8 + item], twin)
+
     def multiply(s, dx, p):
-        item = dx * 2 + p
-
-        def rows_at(i, carry):
-            rows = pl.ds(pl.multiple_of(i * LANES, LANES), LANES)
-            acc = jnp.zeros((LANES, 2 * LANES), jnp.float32)
-            for h in range(2):
-                for k in range(0, HALF, STEP):
-                    ks = pl.ds(k, STEP)
-                    pieces = [
-                        buf[0, dx, 2 * p + i, ks, :] if h == 0 else buf[1, 2 * p + i, dx, ks, :]
-                        for i in range(2)
-                    ]
-                    acc += jnp.dot(
-                        gbuf[s, rows, pl.ds(h * HALF + k, STEP)],
-                        jnp.concatenate(pieces, axis=1),
-                        preferred_element_type=jnp.float32,
-                    )
-            cst[s, item, 0, rows, :] = acc[:, :LANES]
-            cst[s, item, 1, rows, :] = acc[:, LANES:]
+        def body(t, carry):
+            tile(s, dx, p, t)
             return carry
 
-        lax.fori_loop(0, ROWS // LANES, rows_at, 0)
-        send(cst.at[s, item, 1 - mine], xrecv.at[s, item], x_sem.at[s * 8 + item], twin)
+        lax.fori_loop(0, TILES, body, 0)
+        to_other_core(s, dx, p)
 
     given = []
+    ways = (pair, diagonal)
 
     def add_twin(s, dx, p):
         item = dx * 2 + p
@@ -174,8 +190,12 @@
         if s == 0:
             cst[s, item, mine] = total
             copy = pltpu.make_async_remote_copy(
-                pst.at[s, item], rcv.at[0, dx], send_sem.at[len(sent)], rcv_sem.at[dx],
-                device_id=opposite, device_id_type=MESH,
+                pst.at[s, item],
+                rcv.at[0, dx],
+                send_sem.at[len(sent)],
+                rcv_sem.at[dx],
+                device_id=opposite,
+                device_id_type=MESH,
             )
             sent.append(None)
 
@@ -206,6 +226,16 @@
         lanes = pl.ds(pl.multiple_of((chunk + 1 - yl) * LANES, LANES), LANES)
         out_ref[:, lanes] = other.astype(jnp.bfloat16)
 
+    def relay_tests(a):
+        for h in range(2):
+            tests_arrived(h, a, 1)
+            tests_arrived(h, a, 3)
+            test_hop(h, 1, a, 1, 1, part=0)
+            test_hop(h, 1, a, 3, -1, part=1)
+
+    def gradients(t):
+        landed(gbuf.at[1, pl.ds(t * TILE, TILE)], g_sem.at[t])
+
     each(1, 0)
     each(3, 0)
     for h in range(2):
@@ -239,6 +269,9 @@
             hop(h, 1, a, 3, -1, part=1)
         if a == 1:
             multiply(0, 1, 0)
+            gradients(0)
+            tile(1, 0, 0, 0)
+            tile(1, 1, 0, 0)
     for a in (1, 3):
         for h in range(2):
             tests_arrived(h, a, 0)
@@ -248,33 +281,37 @@
             test_hop(h, 1, 0, a, way, part=a // 2)
     add_twin(0, 1, 0)
     multiply(0, 3, 0)
+    tile(1, 3, 0, 0)
     each(0, 2)
     multiply(0, 0, 1)
+    tile(1, 0, 1, 0)
     add_twin(0, 3, 0)
     each(2, 1)
     each(2, 3)
     for h in range(2):
         hop(h, 1, 2, 1, 1, part=0)
         hop(h, 1, 2, 3, -1, part=1)
-    for h in range(2):
-        tests_arrived(h, 2, 0)
-    for a in (1, 3, 2):
+    for a in (1, 3):
         for h in range(2):
             for way in (1, -1):
                 test_hop(h, 1, a, 0, way)
     add_twin(0, 0, 1)
     each(1, 2)
+    multiply(0, 1, 1)
     multiply(0, 2, 0)
-    multiply(0, 1, 1)
+    tile(1, 1, 1, 0)
+    tile(1, 2, 0, 0)
+    add_twin(0, 1, 1)
     add_twin(0, 2, 0)
-    add_twin(0, 1, 1)
-    ref = gbuf.at[1]
-    pltpu.make_async_remote_copy(
-        ref, ref, send_sem.at[0], g_sem.at[0], device_id=twin, device_id_type=MESH
-    ).wait_recv()
+    for h in range(2):
+        tests_arrived(h, 2, 0)
+        for way in (1, -1):
+            test_hop(h, 1, 2, 0, way)
+    gradients(1)
     before = None
     for now in ((0, 0), (0, 1), (1, 0), (1, 1), (3, 0), (2, 0)):
-        multiply(1, *now)
+        tile(1, *now, 1)
+        to_other_core(1, *now)
         if before is not None:
             add_twin(1, *before)
         before = now
@@ -283,61 +320,72 @@
     add_twin(1, *before)
     multiply(1, 3, 1)
     add_twin(0, 3, 1)
+    add_twin(1, 3, 1)
     finish(0)
-    add_twin(1, 3, 1)
     finish(1)
     each(2, 2)
-    for a in (1, 3, 2):
-        for h in range(2):
-            tests_arrived(h, a, 1)
-            tests_arrived(h, a, 3)
-            test_hop(h, 1, a, 1, 1, part=0)
-            test_hop(h, 1, a, 3, -1, part=1)
     multiply(0, 2, 1)
+    relay_tests(1)
     multiply(1, 2, 1)
+    relay_tests(3)
     add_twin(0, 2, 1)
     add_twin(1, 2, 1)
+    relay_tests(2)
     finish(3)
     for h in range(2):
         for a in range(4):
             tests_arrived(h, a, 2)
     finish(2)
 
-    def score(quarter):
-        def tile(i, carry):
-            rows = pl.ds(pl.multiple_of(quarter * 256 + i * LANES, LANES), LANES)
-            part_scores[quarter, pl.ds(pl.multiple_of(i * LANES, LANES), LANES), :] = (
-                lax.dot_general(
-                    tall[rows, :], out_ref[...], (((1,), (1,)), ((), ())),
-                    preferred_element_type=jnp.float32,
-                )
+    def score(quarter, i):
+        rows = pl.ds(pl.multiple_of(quarter * 256 + i * LANES, LANES), LANES)
+        part_scores[quarter, pl.ds(i * LANES, LANES), :] = lax.dot_general(
+            tall[rows, :], out_ref[...], (((1,), (1,)), ((), ())),
+            preferred_element_type=jnp.float32,
+        )
+
+    def to_twin(quarter, k, i):
+        rows = pl.ds(i * LANES, LANES)
+        send(
+            part_scores.at[quarter, rows], twin_scores.at[k, rows], score_sem.at[k * 2 + i], twin
+        )
+
+    def twin_sum(quarter, k, i):
+        rows = pl.ds(i * LANES, LANES)
+        landed(twin_scores.at[k, rows], score_sem.at[k * 2 + i])
+        return part_scores[quarter, rows, :] + twin_scores[k, rows, :]
+
+    far, near = (1 - yh) * 2, yh * 2
+    for i in range(2):
+        score(far + 1 - c, i)
+        to_twin(far + 1 - c, 0, i)
+    for i in range(2):
+        score(far + c, i)
+        part_scores[far + c, pl.ds(i * LANES, LANES), :] = twin_sum(far + c, 0, i)
+        for k in range(2):
+            rows = pl.ds(i * LANES + k * 64, 64)
+            send(
+                part_scores.at[far + c, rows], relay_scores.at[i, k],
+                score_sem.at[4 + i * 2 + k], ways[i],
             )
-            return carry
-
-        lax.fori_loop(0, 2, tile, 0)
-
-    def twin_sum(quarter, k):
-        ref = twin_scores.at[k]
-        pltpu.make_async_remote_copy(
-            ref, ref, send_sem.at[0], score_sem.at[k], device_id=twin, device_id_type=MESH
-        ).wait_recv()
-        return part_scores[quarter] + twin_scores[k]
-
-    far, near = (1 - yh) * 2, yh * 2
-    score(far + 1 - c)
-    send(part_scores.at[far + 1 - c], twin_scores.at[0], score_sem.at[0], twin)
-    score(far + c)
-    part_scores[far + c] = twin_sum(far + c, 0)
-    send(part_scores.at[far + c], far_scores, score_sem.at[2], opposite)
-    score(near + 1 - c)
-    send(part_scores.at[near + 1 - c], twin_scores.at[1], score_sem.at[1], twin)
-    score(near + c)
-    total = twin_sum(near + c, 1)
-    pltpu.make_async_remote_copy(
-        far_scores, far_scores, send_sem.at[0], score_sem.at[2], device_id=twin,
-        device_id_type=MESH,
-    ).wait_recv()
-    score_ref[...] = (total + far_scores[...]) * w_ref[...]
+    for i in range(2):
+        score(near + 1 - c, i)
+        to_twin(near + 1 - c, 1, i)
+    for k in range(2):
+        for i in range(2):
+            landed(relay_scores.at[i, k], score_sem.at[4 + i * 2 + k])
+            send(
+                relay_scores.at[i, k], far_scores.at[i, k], score_sem.at[8 + i * 2 + k],
+                ways[1 - i],
+            )
+        score(near + c, k)
+    for i in range(2):
+        score_ref[pl.ds(i * LANES, LANES), :] = twin_sum(near + c, 1, i)
+    for k in range(2):
+        for i in range(2):
+            landed(far_scores.at[i, k], score_sem.at[8 + i * 2 + k])
+            rows = pl.ds(i * LANES + k * 64, 64)
+            score_ref[rows, :] = score_ref[rows, :] + far_scores[i, k]
     for copy in sent:
         if copy is not None:
             copy.wait_send()
@@ -349,14 +397,13 @@
 
 def local(train_grads, projection, test_features, example_weights):
     flops = 2 * 2 * ROWS * DEPTH * 2048
-    return pl.pallas_call(
+    inner, projected = pl.pallas_call(
         project_kernel,
         out_shape=(
             jax.ShapeDtypeStruct((256, ROWS), jnp.float32),
             jax.ShapeDtypeStruct((ROWS, 1024), jnp.bfloat16),
         ),
-        in_specs=[pl.BlockSpec(memory_space=pl.ANY)] * 3
-        + [pl.BlockSpec(memory_space=pltpu.VMEM)],
+        in_specs=[pl.BlockSpec(memory_space=pltpu.HBM)] * 3,
         out_specs=(pl.BlockSpec(memory_space=pltpu.VMEM),) * 2,
         scratch_shapes=[
             pltpu.VMEM((2, 4, 4, HALF, LANES), jnp.bfloat16),
@@ -368,23 +415,25 @@
             pltpu.VMEM((1024, 1024), jnp.bfloat16),
             pltpu.VMEM((4, 256, ROWS), jnp.float32),
             pltpu.VMEM((2, 256, ROWS), jnp.float32),
-            pltpu.VMEM((256, ROWS), jnp.float32),
+            pltpu.VMEM((2, 2, 64, ROWS), jnp.float32),
+            pltpu.VMEM((2, 2, 64, ROWS), jnp.float32),
             pltpu.SemaphoreType.DMA((4,)),
-            pltpu.SemaphoreType.DMA((136,)),
+            pltpu.SemaphoreType.DMA((160,)),
             pltpu.SemaphoreType.DMA((32,)),
-            pltpu.SemaphoreType.DMA((1,)),
+            pltpu.SemaphoreType.DMA((TILES,)),
             pltpu.SemaphoreType.DMA((16,)),
             pltpu.SemaphoreType.DMA((12,)),
             pltpu.SemaphoreType.DMA((32,)),
-            pltpu.SemaphoreType.DMA((3,)),
+            pltpu.SemaphoreType.DMA((12,)),
         ],
         compiler_params=pltpu.CompilerParams(
-            collective_id=0, has_side_effects=True, vmem_limit_bytes=60 * 1024 * 1024
+            collective_id=0, has_side_effects=True, vmem_limit_bytes=44 * 1024 * 1024
         ),
         cost_estimate=pl.CostEstimate(
             flops=flops, bytes_accessed=8 * 2**20, transcendentals=0
         ),
-    )(train_grads, projection, test_features, example_weights.reshape(1, ROWS))
+    )(*[pltpu.with_memory_space_constraint(v, pltpu.HBM) for v in (train_grads, projection, test_features)])
+    return inner * example_weights[None, :], projected
 
 
 def solution(mesh):

time: 148 us -> 130 us (0.88)
  the two profiles are of different devices: /device:TPU:45 before, /device:TPU:1 now
where the time goes in v3:
time: 130 us
  Pallas kernels  127 us (98%)
    pallas_call x1, Pallas kernels, local(): pl.pallas_call(project_kernel, out_shape=(jax.ShapeDtypeStruct((256, ROWS...  127 us

profile of v3, /device:TPU:1, one launch (start us, length us, event | category | flops | bytes accessed | tf_op | source)
XLA Modules:
  0.0 129.8 jit_solution(11132861312639358499)
XLA Ops:
  0.6 0.0 copy-start
  0.6 127.5 %shard_map.59 = (f32[256,384]{1,0:T(8,128)S(1)}, bf16[384,1024]{1,0:T(8,128)(2,1)S(1)}) custom-call(bf16[384,4096]{1,0:T(8,128)(2,1)} %g_hbm.1, bf16[4096,128]{1,0:T(8,128)(2,1)} %r_hbm.1, bf16[32,1024]{1,0:T(8,128)(2,1)} %t_hbm.1), custom_call_target="tpu_custom_call" | custom-call | flops 12884901888 | bytes 8388608 | tf_op jit(solution)/shard_map/pallas_call | solution.py:400
  128.1 0.0 copy-done
  128.1 0.8 broadcast_multiply_fusion
  128.9 0.9 copy.7
Async XLA Ops:
  0.6 127.5 %copy-start = (f32[384]{0:T(512)S(1)}, f32[384]{0:T(512)}, u32[]{:S(2)}) copy-start(f32[384]{0:T(512)} %param.7) | copy-start | bytes 4612

commit v4 on v3

--- a/solution.py
+++ b/solution.py
@@ -19,7 +19,7 @@
 
 def project_kernel(
     g_hbm, r_hbm, t_hbm, score_ref, out_ref, buf, gbuf, cst, xrecv, pst, rcv,
-    tall, part_scores, twin_scores, relay_scores, far_scores,
+    tall, part_scores, twin_scores, away_scores, relay_scores, far_scores,
     local_sem, send_sem, piece_sem, g_sem, x_sem, rcv_sem, t_sem, score_sem,
 ):
     ex = lax.axis_index("ex")
@@ -361,11 +361,12 @@
         to_twin(far + 1 - c, 0, i)
     for i in range(2):
         score(far + c, i)
-        part_scores[far + c, pl.ds(i * LANES, LANES), :] = twin_sum(far + c, 0, i)
+        total = twin_sum(far + c, 0, i).astype(jnp.bfloat16)
         for k in range(2):
-            rows = pl.ds(i * LANES + k * 64, 64)
+            away_scores[i, k] = total[k * 64 : k * 64 + 64]
+        for k in range(2):
             send(
-                part_scores.at[far + c, rows], relay_scores.at[i, k],
+                away_scores.at[i, k], relay_scores.at[i, k],
                 score_sem.at[4 + i * 2 + k], ways[i],
             )
     for i in range(2):
@@ -385,7 +386,7 @@
         for i in range(2):
             landed(far_scores.at[i, k], score_sem.at[8 + i * 2 + k])
             rows = pl.ds(i * LANES + k * 64, 64)
-            score_ref[rows, :] = score_ref[rows, :] + far_scores[i, k]
+            score_ref[rows, :] = score_ref[rows, :] + far_scores[i, k].astype(jnp.float32)
     for copy in sent:
         if copy is not None:
             copy.wait_send()
@@ -415,8 +416,9 @@
             pltpu.VMEM((1024, 1024), jnp.bfloat16),
             pltpu.VMEM((4, 256, ROWS), jnp.float32),
             pltpu.VMEM((2, 256, ROWS), jnp.float32),
-            pltpu.VMEM((2, 2, 64, ROWS), jnp.float32),
-            pltpu.VMEM((2, 2, 64, ROWS), jnp.float32),
+            pltpu.VMEM((2, 2, 64, ROWS), jnp.bfloat16),
+            pltpu.VMEM((2, 2, 64, ROWS), jnp.bfloat16),
+            pltpu.VMEM((2, 2, 64, ROWS), jnp.bfloat16),
             pltpu.SemaphoreType.DMA((4,)),
             pltpu.SemaphoreType.DMA((160,)),
             pltpu.SemaphoreType.DMA((32,)),

time: 130 us -> 126 us (0.969)
  Pallas kernels: 127 us -> 123 us
    pallas_call x1, Pallas kernels: 127 us -> 123 us  [local(): pl.pallas_call(project_kernel, out_shape=(jax.ShapeDtypeStruct((256, ROWS...]
where the time goes in v4:
time: 126 us; the launch traced here: 125 us
  Pallas kernels  123 us (98%)
    pallas_call x1, Pallas kernels, local(): pl.pallas_call(project_kernel, out_shape=(jax.ShapeDtypeStruct((256, ROWS...  123 us

profile of v4, /device:TPU:1, one launch (start us, length us, event | category | flops | bytes accessed | tf_op | source)
XLA Modules:
  0.0 125.3 jit_solution(5962573452638709406)
XLA Ops:
  0.6 0.0 copy-start
  0.6 123.0 %shard_map.59 = (f32[256,384]{1,0:T(8,128)S(1)}, bf16[384,1024]{1,0:T(8,128)(2,1)S(1)}) custom-call(bf16[384,4096]{1,0:T(8,128)(2,1)} %g_hbm.1, bf16[4096,128]{1,0:T(8,128)(2,1)} %r_hbm.1, bf16[32,1024]{1,0:T(8,128)(2,1)} %t_hbm.1), custom_call_target="tpu_custom_call" | custom-call | flops 12884901888 | bytes 8388608 | tf_op jit(solution)/shard_map/pallas_call | solution.py:401
  123.6 0.0 copy-done
  123.6 0.8 broadcast_multiply_fusion
  124.4 0.9 copy.7
Async XLA Ops:
  0.6 123.0 %copy-start = (f32[384]{0:T(512)S(1)}, f32[384]{0:T(512)}, u32[]{:S(2)}) copy-start(f32[384]{0:T(512)} %param.7) | copy-start | bytes 4612

commit v5 on v4

--- a/solution.py
+++ b/solution.py
@@ -19,7 +19,7 @@
 
 def project_kernel(
     g_hbm, r_hbm, t_hbm, score_ref, out_ref, buf, gbuf, cst, xrecv, pst, rcv,
-    tall, part_scores, twin_scores, away_scores, relay_scores, far_scores,
+    tall, turned, part_scores, twin_scores, away_scores, relay_scores, far_scores,
     local_sem, send_sem, piece_sem, g_sem, x_sem, rcv_sem, t_sem, score_sem,
 ):
     ex = lax.axis_index("ex")
@@ -223,8 +223,10 @@
         other = rcv[1, dx].astype(jnp.float32) + rcv[2, dx].astype(jnp.float32)
         lanes = pl.ds(pl.multiple_of((chunk + yl) * LANES, LANES), LANES)
         out_ref[:, lanes] = own.astype(jnp.bfloat16)
+        turned[lanes, :] = own.T.astype(jnp.bfloat16)
         lanes = pl.ds(pl.multiple_of((chunk + 1 - yl) * LANES, LANES), LANES)
         out_ref[:, lanes] = other.astype(jnp.bfloat16)
+        turned[lanes, :] = other.T.astype(jnp.bfloat16)
 
     def relay_tests(a):
         for h in range(2):
@@ -321,8 +323,6 @@
     multiply(1, 3, 1)
     add_twin(0, 3, 1)
     add_twin(1, 3, 1)
-    finish(0)
-    finish(1)
     each(2, 2)
     multiply(0, 2, 1)
     relay_tests(1)
@@ -331,6 +331,8 @@
     add_twin(0, 2, 1)
     add_twin(1, 2, 1)
     relay_tests(2)
+    finish(0)
+    finish(1)
     finish(3)
     for h in range(2):
         for a in range(4):
@@ -339,9 +341,8 @@
 
     def score(quarter, i):
         rows = pl.ds(pl.multiple_of(quarter * 256 + i * LANES, LANES), LANES)
-        part_scores[quarter, pl.ds(i * LANES, LANES), :] = lax.dot_general(
-            tall[rows, :], out_ref[...], (((1,), (1,)), ((), ())),
-            preferred_element_type=jnp.float32,
+        part_scores[quarter, pl.ds(i * LANES, LANES), :] = jnp.dot(
+            tall[rows, :], turned[...], preferred_element_type=jnp.float32
         )
 
     def to_twin(quarter, k, i):
@@ -414,6 +415,7 @@
             pltpu.VMEM((2, 8, ROWS, LANES), jnp.bfloat16),
             pltpu.VMEM((3, 4, ROWS, LANES), jnp.bfloat16),
             pltpu.VMEM((1024, 1024), jnp.bfloat16),
+            pltpu.VMEM((1024, ROWS), jnp.bfloat16),
             pltpu.VMEM((4, 256, ROWS), jnp.float32),
             pltpu.VMEM((2, 256, ROWS), jnp.float32),
             pltpu.VMEM((2, 2, 64, ROWS), jnp.bfloat16),

time: 126 us -> 125 us (level)
  no operation moved by 1% of the time
where the time goes in v5:
time: 125 us
  Pallas kernels  123 us (98%)
    pallas_call x1, Pallas kernels, local(): pl.pallas_call(project_kernel, out_shape=(jax.ShapeDtypeStruct((256, ROWS...  123 us

profile of v5, /device:TPU:1, one launch (start us, length us, event | category | flops | bytes accessed | tf_op | source)
XLA Modules:
  0.0 125.0 jit_solution(1264902222380162416)
XLA Ops:
  0.6 0.0 copy-start
  0.6 122.7 %shard_map.59 = (f32[256,384]{1,0:T(8,128)S(1)}, bf16[384,1024]{1,0:T(8,128)(2,1)S(1)}) custom-call(bf16[384,4096]{1,0:T(8,128)(2,1)} %g_hbm.1, bf16[4096,128]{1,0:T(8,128)(2,1)} %r_hbm.1, bf16[32,1024]{1,0:T(8,128)(2,1)} %t_hbm.1), custom_call_target="tpu_custom_call" | custom-call | flops 12884901888 | bytes 8388608 | tf_op jit(solution)/shard_map/pallas_call | solution.py:402
  123.4 0.0 copy-done
  123.4 0.8 broadcast_multiply_fusion
  124.2 0.9 copy.7
Async XLA Ops:
  0.6 122.8 %copy-start = (f32[384]{0:T(512)S(1)}, f32[384]{0:T(512)}, u32[]{:S(2)}) copy-start(f32[384]{0:T(512)} %param.7) | copy-start | bytes 4612

commit v6 on v5

--- a/solution.py
+++ b/solution.py
@@ -373,6 +373,8 @@
     for i in range(2):
         score(near + 1 - c, i)
         to_twin(near + 1 - c, 1, i)
+    for i in range(2):
+        score(near + c, i)
     for k in range(2):
         for i in range(2):
             landed(relay_scores.at[i, k], score_sem.at[4 + i * 2 + k])
@@ -380,7 +382,6 @@
                 relay_scores.at[i, k], far_scores.at[i, k], score_sem.at[8 + i * 2 + k],
                 ways[1 - i],
             )
-        score(near + c, k)
     for i in range(2):
         score_ref[pl.ds(i * LANES, LANES), :] = twin_sum(near + c, 1, i)
     for k in range(2):

time: 125 us -> 125 us (level)
  no operation moved by 1% of the time
where the time goes in v6:
time: 125 us
  Pallas kernels  123 us (98%)
    pallas_call x1, Pallas kernels, local(): pl.pallas_call(project_kernel, out_shape=(jax.ShapeDtypeStruct((256, ROWS...  123 us

profile of v6, /device:TPU:1, one launch (start us, length us, event | category | flops | bytes accessed | tf_op | source)
XLA Modules:
  0.0 125.0 jit_solution(9375053956606558644)
XLA Ops:
  0.6 0.0 copy-start
  0.6 122.7 %shard_map.59 = (f32[256,384]{1,0:T(8,128)S(1)}, bf16[384,1024]{1,0:T(8,128)(2,1)S(1)}) custom-call(bf16[384,4096]{1,0:T(8,128)(2,1)} %g_hbm.1, bf16[4096,128]{1,0:T(8,128)(2,1)} %r_hbm.1, bf16[32,1024]{1,0:T(8,128)(2,1)} %t_hbm.1), custom_call_target="tpu_custom_call" | custom-call | flops 12884901888 | bytes 8388608 | tf_op jit(solution)/shard_map/pallas_call | solution.py:403
  123.4 0.0 copy-done
  123.4 0.8 broadcast_multiply_fusion
  124.2 0.9 copy.7
Async XLA Ops:
  0.6 122.8 %copy-start = (f32[384]{0:T(512)S(1)}, f32[384]{0:T(512)}, u32[]{:S(2)}) copy-start(f32[384]{0:T(512)} %param.7) | copy-start | bytes 4612
